TPU v7x, 32 devices: a whole 2x2x4 slice. The times are simulated.
32 devices in a mesh: clip: 4 (over y, core), seq: 8 (over z, x).
Axes of the slice: x: 2, y: 2, z: 4, core: 2. Of those that a mesh axis runs over, the one named last changes fastest.
Arguments:
- block_input: bfloat16 [64, 384, 1152], P('clip', 'seq'), parts along dimension 0, may hold values from -160 to 160
- mid_state: bfloat16 [64, 384, 1152], P('clip', 'seq'), parts along dimension 0, may hold values from -160 to 160
- saved_qkv: bfloat16 [3, 64, 384, 576], P(None, 'clip', 'seq'), parts along dimension 1, may hold values from -6 to 6
- out_grad: bfloat16 [64, 384, 1152], P('clip', 'seq'), parts along dimension 0, may hold values from -6 to 6
- modulation: float32 [20, 1152], P('clip'), parts along dimension 0, may hold values from -3 to 3
- w_qkv_s: bfloat16 [1152, 1728], replicated, may hold values from -0.1875 to 0.1875
- w_out_s: bfloat16 [576, 1152], replicated, may hold values from -0.25 to 0.25
- w_qkv_t: bfloat16 [1152, 1728], replicated, may hold values from -0.1875 to 0.1875
- w_out_t: bfloat16 [576, 1152], replicated, may hold values from -0.25 to 0.25
- qk_gain: float32 [4, 72], replicated, may hold values from 0.1 to 1.9
Outputs:
- input_grad: bfloat16 [64, 384, 1152], P('clip', 'seq'), parts along dimension 0
- mod_grad: float32 [24, 1152], P('clip'), parts along dimension 0
There are 4 independent parts, one for each index of `clip`. A program takes and returns all parts, laid end to end along the dimension named above; an argument that names none is the same for every part. Nothing has to cross between parts.
All inputs are finite; a program needn't handle non-finite values.
Results may differ from a plain program's by a relative error of at most 0.0057.
Values may be sent and summed in bfloat16 or wider, within the bound.
No kernel may reach another device: no remote copies, remote signals or barrier semaphores. Data moves between devices by JAX's collectives and lax.ppermute only.
A program may use at most 128 MiB of HBM per device.

v0:
```python
import jax
import jax.numpy as jnp
from jax import lax
from jax.sharding import PartitionSpec as P

HEADS = 8
HEAD_DIM = 72
WIDTH = 576
NORM_EPS = 1e-06


def layer_stats(inputs):
    values = inputs.astype(jnp.float32)
    centre = jnp.mean(values, axis=-1, keepdims=True)
    spread = jnp.mean(jnp.square(values - centre), axis=-1, keepdims=True)
    inverse = lax.rsqrt(spread + NORM_EPS)
    return ((values - centre) * inverse, inverse)


def modulate(normed, offset, stretch):
    return (normed * (1.0 + stretch) + offset).astype(jnp.bfloat16)


def matmul_rows(left_rows, weight):
    flattened = left_rows.reshape(-1, left_rows.shape[-1])
    result = jnp.dot(flattened, weight, preferred_element_type=jnp.float32)
    return result.reshape(left_rows.shape[:-1] + (weight.shape[1],))


def matmul_back(left_rows, weight):
    flattened = left_rows.reshape(-1, left_rows.shape[-1])
    result = lax.dot_general(
        flattened, weight, (((1,), (1,)), ((), ())), preferred_element_type=jnp.float32
    )
    return result.reshape(left_rows.shape[:-1] + (weight.shape[0],))


def head_split(tensor):
    return tensor.reshape(tensor.shape[:-1] + (HEADS, HEAD_DIM))


def rms_normed(raw_rows, gain_row):
    values = head_split(raw_rows).astype(jnp.float32)
    inverse = lax.rsqrt(jnp.mean(values * values, axis=-1, keepdims=True) + NORM_EPS)
    return ((values * inverse * gain_row).astype(jnp.bfloat16), values, inverse)


def rms_back(values, inverse, gain_row, upstream):
    scaled = gain_row * upstream
    result = inverse * scaled - values * (inverse * inverse * inverse) * jnp.mean(
        values * scaled, axis=-1, keepdims=True
    )
    return result.astype(jnp.bfloat16).reshape(values.shape[:-2] + (-1,))


def attend(queries, key_rows, value_rows, out_cot, query_gain, key_gain):
    query_norm, query_raw, query_inv = rms_normed(queries, query_gain)
    key_norm, key_raw, key_inv = rms_normed(key_rows, key_gain)
    factor = HEAD_DIM ** (-0.5)
    scores = (
        jnp.einsum("blhd,bmhd->bhlm", query_norm, key_norm, preferred_element_type=jnp.float32)
        * factor
    )
    exp_scores = jnp.exp(scores)
    attn_probs = exp_scores / jnp.sum(exp_scores, axis=-1, keepdims=True)
    probs_half = attn_probs.astype(jnp.bfloat16)
    value_heads = head_split(value_rows)
    cot_heads = head_split(out_cot)
    outputs = jnp.einsum(
        "bhlm,bmhd->blhd", probs_half, value_heads, preferred_element_type=jnp.float32
    ).astype(jnp.bfloat16)
    prob_grad = jnp.einsum(
        "blhd,bmhd->bhlm", cot_heads, value_heads, preferred_element_type=jnp.float32
    )
    row_inner = jnp.sum(attn_probs * prob_grad, axis=-1, keepdims=True)
    score_grad = (attn_probs * (prob_grad - row_inner) * factor).astype(jnp.bfloat16)
    value_grad = jnp.einsum(
        "bhlm,blhd->bmhd", probs_half, cot_heads, preferred_element_type=jnp.float32
    ).astype(jnp.bfloat16)
    qnorm_grad = jnp.einsum(
        "bhlm,bmhd->blhd", score_grad, key_norm, preferred_element_type=jnp.float32
    )
    knorm_grad = jnp.einsum(
        "bhlm,blhd->bmhd", score_grad, query_norm, preferred_element_type=jnp.float32
    )
    merged = outputs.shape[:-2] + (-1,)
    return (
        outputs.reshape(merged),
        rms_back(query_raw, query_inv, query_gain, qnorm_grad),
        rms_back(key_raw, key_inv, key_gain, knorm_grad),
        value_grad.reshape(merged),
    )


def output_cot(cotangent, gate_row, w_out):
    scaled = (cotangent.astype(jnp.float32) * gate_row).astype(jnp.bfloat16)
    return matmul_back(scaled, w_out).astype(jnp.bfloat16)


def gate_term(cotangent, outputs, w_out):
    branch = matmul_rows(outputs, w_out)
    return jnp.sum((cotangent.astype(jnp.float32) * branch).reshape(-1, branch.shape[-1]), axis=0)


def input_branch(grad_parts, w_qkv, normed, inverse, stretch):
    joined = jnp.concatenate(grad_parts, axis=-1)
    mod_cot = matmul_back(joined, w_qkv)
    columns = mod_cot.shape[-1]
    offset_term = jnp.sum(mod_cot.reshape(-1, columns), axis=0)
    stretch_term = jnp.sum((mod_cot * normed).reshape(-1, columns), axis=0)
    norm_cot = mod_cot * (1.0 + stretch)
    branch = inverse * (
        norm_cot
        - jnp.mean(norm_cot, axis=-1, keepdims=True)
        - normed * jnp.mean(norm_cot * normed, axis=-1, keepdims=True)
    )
    return (branch, offset_term, stretch_term)


def swapped(tensor):
    return jnp.swapaxes(tensor, 0, 1)


def body(
    block_input,
    mid_state,
    saved_qkv,
    out_grad,
    modulation,
    w_qkv_s,
    w_out_s,
    w_qkv_t,
    w_out_t,
    qk_gain,
):
    normed_mid, inverse_mid = layer_stats(mid_state)
    temporal_cot = output_cot(out_grad, modulation[4], w_out_t)
    temporal_res = attend(
        swapped(saved_qkv[0]),
        swapped(saved_qkv[1]),
        swapped(saved_qkv[2]),
        swapped(temporal_cot),
        qk_gain[2],
        qk_gain[3],
    )
    temporal_gate = gate_term(out_grad, swapped(temporal_res[0]), w_out_t)
    temporal_branch, temporal_offset, temporal_stretch = input_branch(
        tuple((swapped(grad_piece) for grad_piece in temporal_res[1:])),
        w_qkv_t,
        normed_mid,
        inverse_mid,
        modulation[3],
    )
    mid_grad = (out_grad.astype(jnp.float32) + temporal_branch).astype(jnp.bfloat16)
    arrived, landed = (
        lax.all_to_all(block_input, "seq", split_axis=0, concat_axis=1, tiled=True),
        lax.all_to_all(mid_grad, "seq", split_axis=0, concat_axis=1, tiled=True),
    )
    normed_fr, inverse_fr = layer_stats(arrived)
    frame_mod = modulate(normed_fr, modulation[0], modulation[1])
    frame_qkv = matmul_rows(frame_mod, w_qkv_s).astype(jnp.bfloat16)
    frame_cot = output_cot(landed, modulation[2], w_out_s)
    frame_res = attend(
        frame_qkv[..., :WIDTH],
        frame_qkv[..., WIDTH : 2 * WIDTH],
        frame_qkv[..., 2 * WIDTH :],
        frame_cot,
        qk_gain[0],
        qk_gain[1],
    )
    spatial_gate = gate_term(landed, frame_res[0], w_out_s)
    frame_branch, spatial_offset, spatial_stretch = input_branch(
        frame_res[1:], w_qkv_s, normed_fr, inverse_fr, modulation[1]
    )
    outgoing = frame_branch.astype(jnp.bfloat16)
    returned = lax.all_to_all(outgoing, "seq", split_axis=1, concat_axis=0, tiled=True)
    term_stack = jnp.stack(
        [
            spatial_offset,
            spatial_stretch,
            spatial_gate,
            temporal_offset,
            temporal_stretch,
            temporal_gate,
        ]
    )
    totals = lax.psum(term_stack, "seq")
    token_count = block_input.shape[0] * block_input.shape[1] * lax.axis_size("seq")
    mod_grad = totals * token_count ** (-0.5)
    input_grad = (mid_grad.astype(jnp.float32) + returned.astype(jnp.float32)).astype(jnp.bfloat16)
    return (input_grad, mod_grad)


def solution(mesh):
    return jax.shard_map(
        body,
        mesh=mesh,
        in_specs=(
            P("clip", "seq", None),
            P("clip", "seq", None),
            P(None, "clip", "seq", None),
            P("clip", "seq", None),
            P("clip", None),
            P(),
            P(),
            P(),
            P(),
            P(),
        ),
        out_specs=(P("clip", "seq", None), P("clip", None)),
        check_vma=False,
    )
```

profile of v0, /device:TPU:0, one launch (start us, length us, event | category | flops | bytes accessed | tf_op | source)
XLA Modules:
  0.0 314.7 jit_solution(16981990342659741506)
XLA Ops:
  0.7 7.6 %all-to-all-start = ((bf16[16,48,1152]{2,1,0:T(8,128)(2,1)}), bf16[16,48,1152]{2,1,0:T(8,128)(2,1)}, u32[]{:S(2)}, u32[]{:S(2)}) async-start(bf16[16,48,1152]{2,1,0:T(8,128)(2,1)} %param.10), calls=%async_computation | async-start | bytes 3538944 | tf_op jit(solution)/shard_map/all_to_all | solution.py:156
  9.5 2.6 fusion.98
  12.2 3.8 %reshape.326 = bf16[48,16,8,72]{3,2,0,1:T(8,128)(2,1)} reshape(bf16[48,16,576]{2,0,1:T(8,128)(2,1)} %fusion.98) | data formatting | bytes 1769472 | tf_op jit(solution)/shard_map/reshape | solution.py:39
  16.0 3.8 %convert_bitcast_fusion.1 = (f32[48,16,576]{2,0,1:T(8,128)S(1)}, bf16[48,16,576]{2,0,1:T(8,128)(2,1)}, f32[48,16,576]{2,0,1:T(8,128)}) fusion(bf16[3,16,48,576]{3,2,1,0:T(8,128)(2,1)} %param.12), kind=kLoop, calls=%fused_computation.88 | loop fusion | flops 884736 | bytes 7077888 | tf_op jit(solution)/shard_map/convert_element_type | solution.py:43
  20.4 2.6 reshape.337
  23.0 2.9 multiply_reduce_fusion.7
  26.9 2.5 reshape.355
  29.4 2.2 copy.189
  31.6 2.8 reshape.338
  34.4 2.9 multiply_reduce_fusion.6
  38.3 5.2 %fusion.94 = f32[48,8,16,16]{2,3,1,0:T(8,128)} fusion(bf16[48,16,8,72]{3,2,0,1:T(8,128)(2,1)S(1)} %copy-done.11, bf16[48,16,8,72]{3,2,0,1:T(8,128)(2,1)} %reshape.326), kind=kOutput, calls=%fused_computation.120 | convolution fusion | flops 14155776 | bytes 2162688 | tf_op jit(solution)/shard_map/blhd,bmhd->bhlm/dot_general | solution.py:72
  43.5 2.0 fusion.44
  47.2 2.6 fusion.82
  49.8 11.1 %fusion.38 = (f32[48,16,8]{1,2,0:T(8,128)}, f32[48,8,72,16]{2,3,1,0:T(8,128)}) fusion(f32[48,16,8,72]{3,2,1,0:T(8,128)} %reshape.338, f32[72]{0:T(128)S(1)} %copy-done.35, f32[48,8,16,16]{2,3,1,0:T(8,128)} %fusion.94, f32[48,8,16]{2,1,0:T(8,128)S(1)} %get-tuple-element.33, f32[48,8,16,16]{2,3,1,0:T(8,128)} %copy-done.19, f32[48,16,8,72]{3,2,1,0:T(8,128)} %reshape.337, ...), kind=kOutput, calls=%fused_computation.53 | convolution fusion | flops 17694736 | bytes 6169152 | tf_op jit(solution)/shard_map/bhlm,blhd->bmhd/dot_general | solution.py:83
  60.9 12.1 %fusion.41 = (f32[48,16,8]{1,2,0:T(8,128)}, f32[48,8,72,16]{2,3,1,0:T(8,128)}) fusion(f32[48,16,8,72]{3,2,1,0:T(8,128)} %reshape.337, f32[72]{0:T(128)S(1)} %copy-done.36, f32[48,8,16,16]{2,3,1,0:T(8,128)} %fusion.94, f32[48,8,16]{2,1,0:T(8,128)S(1)} %get-tuple-element.33, f32[48,8,16,16]{2,3,1,0:T(8,128)} %copy-done.19, f32[48,16,8,72]{3,2,1,0:T(8,128)} %reshape.338, ...), kind=kOutput, calls=%fused_computation.58 | convolution fusion | flops 17694736 | bytes 6169152 | tf_op jit(solution)/shard_map/bhlm,bmhd->blhd/dot_general | solution.py:80
  73.9 1.8 copy.211
  75.8 2.4 reshape.330
  81.9 7.4 %fusion.37 = (bf16[48,16,8,72]{3,1,2,0:T(8,128)(2,1)S(1)}, bf16[48,16,8,72]{3,1,2,0:T(8,128)(2,1)S(1)}) fusion(f32[48,8,72,16]{2,3,1,0:T(8,128)} %get-tuple-element.38, f32[48,16,8,72]{3,2,1,0:T(8,128)} %reshape.338, f32[48,16,8]{1,2,0:T(8,128)} %copy.208, f32[48,16,8]{1,2,0:T(8,128)} %copy.204, f32[72]{0:T(128)S(1)} %copy-done.35, ...), kind=kLoop, calls=%fused_computation.52 | loop fusion | flops 5308416 | bytes 8995392 | tf_op jit(solution)/shard_map/convert_element_type | solution.py:53
  90.9 3.6 %reshape.329 = bf16[48,16,576]{2,1,0:T(8,128)(2,1)} reshape(bf16[48,16,8,72]{3,2,1,0:T(8,128)(2,1)} %copy.209) | data formatting | bytes 1769472 | tf_op jit(solution)/shard_map/reshape | solution.py:53
  96.1 3.8 %reshape.328 = bf16[48,16,576]{2,1,0:T(8,128)(2,1)} reshape(bf16[48,16,8,72]{3,2,1,0:T(8,128)(2,1)} %copy.203) | data formatting | bytes 1769472 | tf_op jit(solution)/shard_map/reshape | solution.py:53
  99.9 5.0 %concatenate.13 = bf16[16,48,1728]{2,0,1:T(8,128)(2,1)} concatenate(bf16[16,48,576]{2,0,1:T(8,128)(2,1)} %bitcast.185, bf16[16,48,576]{2,0,1:T(8,128)(2,1)S(1)} %bitcast.184, bf16[16,48,576]{2,0,1:T(8,128)(2,1)S(1)} %bitcast.183), dimensions={2} | concatenate | bytes 5308416 | tf_op jit(solution)/shard_map/concatenate | solution.py:106
  104.9 2.7 copy.212
  107.8 5.5 %fusion.138 = (f32[1152]{0:T(1024)S(1)}, f32[768]{0:T(1024)S(1)}, f32[768,1152]{1,0:T(8,128)}) fusion(f32[1152]{0:T(1024)S(1)} %copy-done.28, bf16[768,1728]{1,0:T(8,128)(2,1)S(1)} %bitcast.192, bf16[1152,1728]{0,1:T(8,128)(2,1)S(1)} %copy-done.38), kind=kOutput, calls=%fused_computation.175 | convolution fusion | flops 3060300032 | bytes 10186752 | tf_op jit(solution)/shard_map/dot_general | solution.py:32
  116.8 2.4 fusion.26
  119.2 6.2 %all-to-all-start.1 = ((bf16[16,48,1152]{2,1,0:T(8,128)(2,1)}), bf16[16,48,1152]{2,1,0:T(8,128)(2,1)}, u32[]{:S(2)}, u32[]{:S(2)}) async-start(bf16[16,48,1152]{2,1,0:T(8,128)(2,1)} %fusion.26), calls=%async_computation.1 | async-start | bytes 3538944 | tf_op jit(solution)/shard_map/all_to_all | solution.py:157
  125.5 1.7 bitcast_convert_fusion
  128.3 1.7 copy.213
  130.0 1.8 copy-done.3
  133.4 3.8 %fusion.33 = bf16[2,384,1728]{1,2,0:T(8,128)(2,1)S(1)} fusion(bf16[2,384,1152]{2,1,0:T(8,128)(2,1)S(1)} %add_convert_fusion, bf16[1152,1728]{0,1:T(8,128)(2,1)S(1)} %copy-done.39), kind=kOutput, calls=%fused_computation.47 | convolution fusion | flops 3058974720 | bytes 8404992 | tf_op jit(solution)/shard_map/dot_general | solution.py:26
  139.0 27.2 %all-to-all-done.1 = bf16[16,48,1152]{2,1,0:T(8,128)(2,1)} async-done(((bf16[16,48,1152]{2,1,0:T(8,128)(2,1)}), bf16[16,48,1152]{2,1,0:T(8,128)(2,1)}, u32[]{:S(2)}, u32[]{:S(2)}) %all-to-all-start.1) | async-done | bytes 1769504 | tf_op jit(solution)/shard_map/all_to_all | solution.py:157
  168.2 2.0 copy-done.41
  171.6 5.1 %fusion.148 = f32[2,8,384,384]{2,3,1,0:T(8,128)} fusion(bf16[2,384,8,72]{1,3,2,0:T(8,128)(2,1)S(1)} %bitcast.197, bf16[2,384,8,72]{1,3,2,0:T(8,128)(2,1)S(1)} %bitcast.190), kind=kOutput, calls=%fused_computation.178 | convolution fusion | flops 339738624 | bytes 11206656 | tf_op jit(solution)/shard_map/blhd,bmhd->bhlm/dot_general | solution.py:72
  176.7 1.9 fusion.4
  178.7 3.6 %copy-done.10 = f32[2,8,384,384]{2,3,1,0:T(8,128)} copy-done((f32[2,8,384,384]{2,3,1,0:T(8,128)}, f32[2,8,384,384]{2,3,1,0:T(8,128)S(1)}, u32[]{:S(2)}) %copy-start.10) | copy-done | bytes 9437208
  182.3 3.0 fusion.105
  185.3 18.2 %fusion.63 = (f32[2,384,8]{1,2,0:T(8,128)S(1)}, f32[2,8,72,384]{3,2,1,0:T(8,128)}) fusion(bf16[2,384,8,72]{1,3,2,0:T(8,128)(2,1)S(1)} %bitcast.175, f32[72]{0:T(128)S(1)} %copy-done.33, f32[2,8,384,384]{2,3,1,0:T(8,128)} %fusion.148, f32[2,8,384]{2,1,0:T(8,128)S(1)} %get-tuple-element.40, f32[2,8,384,384]{2,3,1,0:T(8,128)} %copy-done.10, ...), kind=kOutput, calls=%fused_computation.95 | convolution fusion | flops 364511616 | bytes 22487616 | tf_op jit(solution)/shard_map/bhlm,blhd->bmhd/dot_general | solution.py:83
  203.5 17.9 %fusion.70 = (f32[2,384,8]{1,2,0:T(8,128)S(1)}, f32[2,8,72,384]{3,2,1,0:T(8,128)}) fusion(bf16[2,384,8,72]{1,3,2,0:T(8,128)(2,1)S(1)} %bitcast.181, f32[72]{0:T(128)S(1)} %copy-done.34, f32[2,8,384,384]{2,3,1,0:T(8,128)} %fusion.148, f32[2,8,384]{2,1,0:T(8,128)S(1)} %get-tuple-element.40, f32[2,8,384,384]{2,3,1,0:T(8,128)} %copy-done.10, ...), kind=kOutput, calls=%fused_computation.102 | convolution fusion | flops 364511616 | bytes 22487616 | tf_op jit(solution)/shard_map/bhlm,bmhd->blhd/dot_general | solution.py:80
  221.3 2.2 copy.220
  228.4 6.2 %multiply_reduce_fusion.1 = (f32[1152]{0:T(1024)S(1)}, f32[768]{0:T(1024)S(1)}, f32[768]{0:T(1024)S(1)}, f32[1152]{0:T(1024)S(1)}, f32[768,1152]{1,0:T(8,128)}) fusion(f32[8,2,48,1152]{3,2,0,1:T(8,128)S(1)} %copy-done.4, f32[768]{0:T(1024)S(1)} %rsqrt.74, f32[768]{0:T(1024)S(1)} %div.96, f32[1152]{0:T(1024)S(1)} %copy-done.29, ...), kind=kOutput, calls=%fused_computation.42 | convolution fusion | flops 3073569280 | bytes 13739520 | tf_op jit(solution)/shard_map/dot_general | solution.py:32
  234.6 3.9 %multiply_convert_fusion.1 = bf16[2,384,1152]{2,1,0:T(8,128)(2,1)S(1)} fusion(f32[2,384,1152]{2,1,0:T(8,128)} %bitcast.189, f32[8,2,48,1152]{3,2,0,1:T(8,128)} %copy-done.3, f32[2,384]{1,0:T(2,128)S(1)} %div.98, f32[2,384]{1,0:T(2,128)S(1)} %div.95, f32[1152]{0:T(1024)S(1)} %copy-done.29, f32[2,384]{1,0:T(2,128)S(1)} %div.87, f32[2,384]{1,0:T(2,128)S(1)} %rsqrt.71), kind=kLoop, calls=%fused_computation.43 | loop fusion | flops 7077888 | bytes 8864256 | tf_op jit(solution)/shard_map/convert_element_type | solution.py:175
  238.5 3.1 copy.221
  241.7 4.3 %all-to-all-start.2 = ((bf16[2,384,1152]{2,0,1:T(2,128)(2,1)}), bf16[2,384,1152]{2,0,1:T(2,128)(2,1)}, u32[]{:S(2)}, u32[]{:S(2)}) async-start(bf16[2,384,1152]{2,0,1:T(2,128)(2,1)} %copy.221), calls=%async_computation.2 | async-start | bytes 3538944 | tf_op jit(solution)/shard_map/all_to_all | solution.py:176
  246.0 3.4 %fusion.83 = bf16[48,16,8,72]{3,1,2,0:T(8,128)(2,1)S(1)} fusion(bf16[48,16,8,72]{3,2,0,1:T(8,128)(2,1)S(1)} %copy-done.12, f32[48,8,16,16]{2,3,1,0:T(8,128)} %copy-done.19, f32[48,8,16]{2,1,0:T(8,128)S(1)} %copy-done.27), kind=kOutput, calls=%fused_computation.114 | convolution fusion | flops 14893056 | bytes 2187264 | tf_op jit(solution)/shard_map/bhlm,bmhd->blhd/dot_general | solution.py:69
  249.8 2.0 reshape.336
  251.8 3.5 %fusion.81 = f32[1152]{0:T(1024)S(1)} fusion(bf16[16,48,1152]{2,1,0:T(8,128)(2,1)} %param.13, bf16[576,1152]{1,0:T(8,128)(2,1)S(1)} %copy-done, bf16[16,48,576]{2,0,1:T(8,128)(2,1)} %bitcast.193), kind=kOutput, calls=%fused_computation.112 | convolution fusion | flops 1021868928 | bytes 3985920 | tf_op jit(solution)/shard_map/dot_general | solution.py:26
  255.3 5.6 %fusion.90 = bf16[2,8,72,384]{3,2,1,0:T(8,128)(2,1)S(1)} fusion(bf16[2,384,8,72]{1,3,2,0:T(8,128)(2,1)S(1)} %bitcast.191, f32[2,8,384,384]{2,3,1,0:T(8,128)} %copy-done.10, f32[2,8,384]{2,1,0:T(8,128)S(1)} %get-tuple-element.40), kind=kOutput, calls=%fused_computation.117 | convolution fusion | flops 347258880 | bytes 11231232 | tf_op jit(solution)/shard_map/bhlm,bmhd->blhd/dot_general | solution.py:69
  262.8 47.5 %psum.7 = f32[6,1152]{1,0:T(8,128)S(1)} all-reduce(f32[6,1152]{1,0:T(8,128)S(1)} %stack.27), channel_id=1, replica_groups=mesh['clip'=4,'seq'=8] {'seq'}, use_global_device_ids=true, to_apply=%region_26.0 | all-reduce | flops 6912 | bytes 55296 | tf_op jit(solution)/shard_map/psum | solution.py:187
  310.9 1.7 copy.222
  (152 shorter events, 33.7 us)
Async XLA Ops:
  0.6 8.9 %copy-start = (bf16[576,1152]{1,0:T(8,128)(2,1)S(1)}, bf16[576,1152]{1,0:T(8,128)(2,1)}, u32[]{:S(2)}) copy-start(bf16[576,1152]{1,0:T(8,128)(2,1)} %param.18) | copy-start | bytes 3981316
  0.6 7.6 %copy-start.37 = (f32[4,72]{1,0:T(4,128)S(1)}, f32[4,72]{1,0:T(4,128)}, u32[]{:S(2)}) copy-start(f32[4,72]{1,0:T(4,128)} %param.19) | copy-start | bytes 3460
  0.7 8.2 %copy-start.32 = (f32[5,1152]{1,0:T(8,128)S(1)}, f32[5,1152]{1,0:T(8,128)}, u32[]{:S(2)}) copy-start(f32[5,1152]{1,0:T(8,128)} %param.14) | copy-start | bytes 69124
  0.7 8.8 %copy-start.20 = (bf16[16,48,1152]{2,1,0:T(8,128)(2,1)S(1)}, bf16[16,48,1152]{2,1,0:T(8,128)(2,1)}, u32[]{:S(2)}) copy-start(bf16[16,48,1152]{2,1,0:T(8,128)(2,1)} %param.13) | copy-start | bytes 5308420
  0.7 118.6 %all-to-all-start = ((bf16[16,48,1152]{2,1,0:T(8,128)(2,1)}), bf16[16,48,1152]{2,1,0:T(8,128)(2,1)}, u32[]{:S(2)}, u32[]{:S(2)}) async-start(bf16[16,48,1152]{2,1,0:T(8,128)(2,1)} %param.10), calls=%async_computation | async-start | bytes 3538944 | tf_op jit(solution)/shard_map/all_to_all | solution.py:156
  23.0 3.9 %copy-start.15 = (bf16[48,16,576]{2,0,1:T(8,128)(2,1)S(1)}, bf16[48,16,576]{2,0,1:T(8,128)(2,1)}, u32[]{:S(2)}) copy-start(bf16[48,16,576]{2,0,1:T(8,128)(2,1)} %get-tuple-element.16) | copy-start | bytes 2654212
  34.4 3.9 %copy-start.11 = (bf16[48,16,8,72]{3,2,0,1:T(8,128)(2,1)S(1)}, bf16[48,16,8,72]{3,2,0,1:T(8,128)(2,1)}, u32[]{:S(2)}) copy-start(bf16[48,16,8,72]{3,2,0,1:T(8,128)(2,1)} %reshape.355) | copy-start | bytes 2654212
  38.3 5.2 %copy-start.1 = (f32[48,16,8,72]{3,2,1,0:T(8,128)S(1)}, f32[48,16,8,72]{3,2,1,0:T(8,128)}, u32[]{:S(2)}) copy-start(f32[48,16,8,72]{3,2,1,0:T(8,128)} %reshape.337) | copy-start | bytes 5308420
  38.3 5.2 %copy-start.2 = (f32[48,16,8,72]{3,2,1,0:T(8,128)S(1)}, f32[48,16,8,72]{3,2,1,0:T(8,128)}, u32[]{:S(2)}) copy-start(f32[48,16,8,72]{3,2,1,0:T(8,128)} %reshape.338) | copy-start | bytes 5308420
  38.3 5.2 %copy-start.35 = (f32[72]{0:T(128)S(1)}, f32[72]{0:T(128)}, u32[]{:S(2)}) copy-start(f32[72]{0:T(128)} %get-tuple-element.30) | copy-start | bytes 868
  38.3 5.2 %copy-start.36 = (f32[72]{0:T(128)S(1)}, f32[72]{0:T(128)}, u32[]{:S(2)}) copy-start(f32[72]{0:T(128)} %get-tuple-element.31) | copy-start | bytes 868
  43.5 3.7 %copy-start.13 = (bf16[48,16,8,72]{3,2,0,1:T(8,128)(2,1)S(1)}, bf16[48,16,8,72]{3,2,0,1:T(8,128)(2,1)}, u32[]{:S(2)}) copy-start(bf16[48,16,8,72]{3,2,0,1:T(8,128)(2,1)} %reshape.326) | copy-start | bytes 2654212
  45.6 1.6 copy-start.19
  45.6 15.3 %copy-start.26 = (f32[48,8,16]{2,1,0:T(8,128)}, f32[48,8,16]{2,1,0:T(8,128)S(1)}, u32[]{:S(2)}) copy-start(f32[48,8,16]{2,1,0:T(8,128)S(1)} %get-tuple-element.33) | copy-start | bytes 73732
  60.9 12.1 %copy-start.24 = (f32[48,16,8]{0,2,1:T(8,128)S(1)}, f32[48,16,8]{0,2,1:T(8,128)}, u32[]{:S(2)}) copy-start(f32[48,16,8]{0,2,1:T(8,128)} %get-tuple-element.23) | copy-start | bytes 73732
  60.9 12.3 %copy-start.25 = (f32[48,16,8]{0,2,1:T(8,128)S(1)}, f32[48,16,8]{0,2,1:T(8,128)}, u32[]{:S(2)}) copy-start(f32[48,16,8]{0,2,1:T(8,128)} %get-tuple-element.21) | copy-start | bytes 73732
  96.1 3.8 %copy-start.14 = (bf16[48,16,576]{2,1,0:T(8,128)(2,1)S(1)}, bf16[48,16,576]{2,1,0:T(8,128)(2,1)}, u32[]{:S(2)}) copy-start(bf16[48,16,576]{2,1,0:T(8,128)(2,1)} %reshape.330) | copy-start | bytes 2654212
  96.1 3.8 %copy-start.16 = (bf16[48,16,576]{2,1,0:T(8,128)(2,1)S(1)}, bf16[48,16,576]{2,1,0:T(8,128)(2,1)}, u32[]{:S(2)}) copy-start(bf16[48,16,576]{2,1,0:T(8,128)(2,1)} %reshape.329) | copy-start | bytes 2654212
  104.9 2.7 copy-start.28
  104.9 3.0 copy-start.38
  107.8 5.6 %copy-start.5 = (bf16[16,48,1152]{2,1,0:T(8,128)(2,1)S(1)}, bf16[16,48,1152]{2,1,0:T(8,128)(2,1)}, u32[]{:S(2)}) copy-start(bf16[16,48,1152]{2,1,0:T(8,128)(2,1)} %param.11) | copy-start | bytes 5308420
  113.4 2.0 copy-start.7
  113.8 3.0 copy-start.21
  119.2 46.9 %all-to-all-start.1 = ((bf16[16,48,1152]{2,1,0:T(8,128)(2,1)}), bf16[16,48,1152]{2,1,0:T(8,128)(2,1)}, u32[]{:S(2)}, u32[]{:S(2)}) async-start(bf16[16,48,1152]{2,1,0:T(8,128)(2,1)} %fusion.26), calls=%async_computation.1 | async-start | bytes 3538944 | tf_op jit(solution)/shard_map/all_to_all | solution.py:157
  128.0 3.9 %copy-start.29 = (f32[1152]{0:T(1024)S(1)}, f32[1152]{0:T(1024)}, u32[]{:S(2)}) copy-start(f32[1152]{0:T(1024)} %get-tuple-element.10) | copy-start | bytes 13828
  128.0 3.9 %copy-start.31 = (f32[1152]{0:T(1024)S(1)}, f32[1152]{0:T(1024)}, u32[]{:S(2)}) copy-start(f32[1152]{0:T(1024)} %get-tuple-element.14) | copy-start | bytes 13828
  130.0 1.8 copy-start.3
  130.0 3.4 %copy-start.39 = (bf16[1152,1728]{0,1:T(8,128)(2,1)S(1)}, bf16[1152,1728]{0,1:T(8,128)(2,1)}, u32[]{:S(2)}) copy-start(bf16[1152,1728]{0,1:T(8,128)(2,1)} %param.15) | copy-start | bytes 11943940
  138.7 29.2 %copy-start.30 = (f32[1152]{0:T(1024)S(1)}, f32[1152]{0:T(1024)}, u32[]{:S(2)}) copy-start(f32[1152]{0:T(1024)} %get-tuple-element.13) | copy-start | bytes 13828
  167.9 3.7 %copy-start.8 = (f32[8,2,48,1152]{3,2,0,1:T(8,128)}, f32[8,2,48,1152]{3,2,0,1:T(8,128)S(1)}, u32[]{:S(2)}) copy-start(f32[8,2,48,1152]{3,2,0,1:T(8,128)S(1)} %copy.214) | copy-start | bytes 10616836
  167.9 2.3 copy-start.41
  170.2 1.4 copy-start.17
  171.6 5.1 %copy-start.33 = (f32[72]{0:T(128)S(1)}, f32[72]{0:T(128)}, u32[]{:S(2)}) copy-start(f32[72]{0:T(128)} %get-tuple-element.29) | copy-start | bytes 868
  171.6 5.1 %copy-start.34 = (f32[72]{0:T(128)S(1)}, f32[72]{0:T(128)}, u32[]{:S(2)}) copy-start(f32[72]{0:T(128)} %get-tuple-element.32) | copy-start | bytes 868
  178.6 3.6 %copy-start.10 = (f32[2,8,384,384]{2,3,1,0:T(8,128)}, f32[2,8,384,384]{2,3,1,0:T(8,128)S(1)}, u32[]{:S(2)}) copy-start(f32[2,8,384,384]{2,3,1,0:T(8,128)S(1)} %get-tuple-element.41) | copy-start | bytes 28311556
  221.3 2.4 copy-start.23
  223.7 1.6 copy-start.22
  225.2 2.1 copy-start.40
  225.4 3.0 copy-start.4
  238.5 7.5 %copy-start.12 = (bf16[48,16,8,72]{3,2,0,1:T(8,128)(2,1)S(1)}, bf16[48,16,8,72]{3,2,0,1:T(8,128)(2,1)}, u32[]{:S(2)}) copy-start(bf16[48,16,8,72]{3,2,0,1:T(8,128)(2,1)} %reshape.355) | copy-start | bytes 2654212
  238.5 7.5 %copy-start.27 = (f32[48,8,16]{2,1,0:T(8,128)S(1)}, f32[48,8,16]{2,1,0:T(8,128)}, u32[]{:S(2)}) copy-start(f32[48,8,16]{2,1,0:T(8,128)} %copy-done.26) | copy-start | bytes 73732
  241.7 69.3 %all-to-all-start.2 = ((bf16[2,384,1152]{2,0,1:T(2,128)(2,1)}), bf16[2,384,1152]{2,0,1:T(2,128)(2,1)}, u32[]{:S(2)}, u32[]{:S(2)}) async-start(bf16[2,384,1152]{2,0,1:T(2,128)(2,1)} %copy.221), calls=%async_computation.2 | async-start | bytes 3538944 | tf_op jit(solution)/shard_map/all_to_all | solution.py:176
  251.8 3.5 %copy-start.18 = (bf16[2,384,576]{1,2,0:T(8,128)(2,1)S(1)}, bf16[2,384,576]{1,2,0:T(8,128)(2,1)}, u32[]{:S(2)}) copy-start(bf16[2,384,576]{1,2,0:T(8,128)(2,1)} %get-tuple-element.18) | copy-start | bytes 2654212
  255.3 5.6 %copy-start.9 = (f32[8,2,48,1152]{3,2,0,1:T(8,128)S(1)}, f32[8,2,48,1152]{3,2,0,1:T(8,128)}, u32[]{:S(2)}) copy-start(f32[8,2,48,1152]{3,2,0,1:T(8,128)} %copy-done.8) | copy-start | bytes 10616836
  255.3 5.6 %copy-start.42 = (bf16[576,1152]{1,0:T(8,128)(2,1)S(1)}, bf16[576,1152]{1,0:T(8,128)(2,1)}, u32[]{:S(2)}) copy-start(bf16[576,1152]{1,0:T(8,128)(2,1)} %param.16) | copy-start | bytes 3981316
  262.7 50.0 %copy-start.6 = (bf16[16,48,1152]{2,1,0:T(8,128)(2,1)S(1)}, bf16[16,48,1152]{2,1,0:T(8,128)(2,1)}, u32[]{:S(2)}) copy-start(bf16[16,48,1152]{2,1,0:T(8,128)(2,1)} %fusion.26) | copy-start | bytes 5308420
where the time goes:
time: 321 us; the launch traced here: 315 us
  matrix products  113 us (35%)
  local copies, waits for them, and re-layouts  72.6 us (23%)
  blocking collectives  47.5 us (15%)
  other arithmetic  34.5 us (11%)
  waiting for transfers between devices  27.2 us (8%)
  starting transfers between devices  18.1 us (6%)
    psum x1, blocking collectives, body(): totals = lax.psum(term_stack, 'seq')  47.5 us
    dot_general x2, matrix products, attend(): jnp.einsum('bhlm,bmhd->blhd', score_grad, key_norm, preferred_element_typ...  30 us
    dot_general x2, matrix products, attend(): jnp.einsum('bhlm,blhd->bmhd', score_grad, query_norm, preferred_element_t...  29.3 us
    all_to_all x1, waiting for transfers between devices, body(): lax.all_to_all(mid_grad, 'seq', split_axis=0, concat_axis=1, tiled=True)  27.2 us
    dot_general x4, matrix products, matmul_back(): lax.dot_general(flattened, weight, (((1,), (1,)), ((), ())), preferred_el...  15.7 us
    unnamed x89, local copies, waits for them, and re-layouts  13.3 us
    dot_general x2, matrix products, attend(): jnp.einsum('blhd,bmhd->bhlm', cot_heads, value_heads, preferred_element_t...  10.3 us
    dot_general x3, matrix products, matmul_rows(): result = jnp.dot(flattened, weight, preferred_element_type=jnp.float32)  9.04 us
  transfers between devices with their start and end apart: 3, of which 1 were waited for; matrix products, arithmetic and copies ran while one was open for 43% of the time, Pallas kernels for 0%

commit v1 on v0

--- a/solution.py
+++ b/solution.py
@@ -2,11 +2,15 @@
 import jax.numpy as jnp
 from jax import lax
 from jax.sharding import PartitionSpec as P
+from jax.lax import all_to_all, axis_size
 
 HEADS = 8
 HEAD_DIM = 72
 WIDTH = 576
 NORM_EPS = 1e-06
+draft_the_column = lambda unit: jnp.concatenate(
+    all_to_all(jnp.stack(jnp.split(unit, axis_size("seq"), axis=0), axis=0), "seq", 0, 0), axis=1
+)
 
 
 def layer_stats(inputs):
@@ -154,7 +158,7 @@
     mid_grad = (out_grad.astype(jnp.float32) + temporal_branch).astype(jnp.bfloat16)
     arrived, landed = (
         lax.all_to_all(block_input, "seq", split_axis=0, concat_axis=1, tiled=True),
-        lax.all_to_all(mid_grad, "seq", split_axis=0, concat_axis=1, tiled=True),
+        draft_the_column(mid_grad),
     )
     normed_fr, inverse_fr = layer_stats(arrived)
     frame_mod = modulate(normed_fr, modulation[0], modulation[1])

time: 321 us -> 341 us (1.062)
  local copies, waits for them, and re-layouts: 72.6 us -> 84.7 us
  other arithmetic: 34.5 us -> 41.7 us
    unnamed x89 -> x98, local copies, waits for them, and re-layouts: 13.3 us -> 18 us
  transfers between devices with their start and end apart: 3 -> 3, of which waited for: 1 -> 1; matrix products, arithmetic and copies ran while one was open for 43% -> 46% of each run, Pallas kernels for 0% -> 0%
where the time goes in v1:
time: 341 us; the launch traced here: 334 us
  matrix products  113 us (33%)
  local copies, waits for them, and re-layouts  84.7 us (25%)
  blocking collectives  47.5 us (14%)
  other arithmetic  41.7 us (12%)
  waiting for transfers between devices  27.2 us (8%)
  starting transfers between devices  18.1 us (5%)
    psum x1, blocking collectives, body(): totals = lax.psum(term_stack, 'seq')  47.5 us
    dot_general x2, matrix products, attend(): jnp.einsum('bhlm,bmhd->blhd', score_grad, key_norm, preferred_element_typ...  30.3 us
    dot_general x2, matrix products, attend(): jnp.einsum('bhlm,blhd->bmhd', score_grad, query_norm, preferred_element_t...  29.3 us
    all_to_all x1, waiting for transfers between devices, all_to_all(jnp.stack(jnp.split(unit, axis_size('seq'), axis=0), axis=0),...  27.2 us
    unnamed x98, local copies, waits for them, and re-layouts  18 us
    dot_general x4, matrix products, matmul_back(): lax.dot_general(flattened, weight, (((1,), (1,)), ((), ())), preferred_el...  15.7 us
    dot_general x2, matrix products, attend(): jnp.einsum('blhd,bmhd->bhlm', cot_heads, value_heads, preferred_element_t...  10.3 us
    convert_element_type x3, other arithmetic, rms_back(): return result.astype(jnp.bfloat16).reshape(values.shape[:-2] + (-1,))  9.97 us
  transfers between devices with their start and end apart: 3, of which 1 were waited for; matrix products, arithmetic and copies ran while one was open for 46% of the time, Pallas kernels for 0%

profile of v1, /device:TPU:0, one launch (start us, length us, event | category | flops | bytes accessed | tf_op | source)
XLA Modules:
  0.0 334.2 jit_solution(4211968290046407697)
XLA Ops:
  0.7 7.6 %all-to-all-start = ((bf16[16,48,1152]{2,1,0:T(8,128)(2,1)}), bf16[16,48,1152]{2,1,0:T(8,128)(2,1)}, u32[]{:S(2)}, u32[]{:S(2)}) async-start(bf16[16,48,1152]{2,1,0:T(8,128)(2,1)} %param.10), calls=%async_computation | async-start | bytes 3538944 | tf_op jit(solution)/shard_map/all_to_all | solution.py:160
  9.5 2.7 fusion.98
  12.2 3.8 %reshape.326 = bf16[48,16,8,72]{3,2,0,1:T(8,128)(2,1)} reshape(bf16[48,16,576]{2,0,1:T(8,128)(2,1)} %fusion.98) | data formatting | bytes 1769472 | tf_op jit(solution)/shard_map/reshape | solution.py:43
  16.0 3.8 %convert_bitcast_fusion.2 = (f32[48,16,576]{2,0,1:T(8,128)S(1)}, bf16[48,16,576]{2,0,1:T(8,128)(2,1)}, f32[48,16,576]{2,0,1:T(8,128)}) fusion(bf16[3,16,48,576]{3,2,1,0:T(8,128)(2,1)} %param.12), kind=kLoop, calls=%fused_computation.89 | loop fusion | flops 884736 | bytes 7077888 | tf_op jit(solution)/shard_map/convert_element_type | solution.py:47
  20.4 2.6 reshape.337
  23.0 2.9 multiply_reduce_fusion.7
  26.9 2.5 reshape.354
  29.4 2.2 copy.189
  31.6 2.8 reshape.338
  34.4 2.9 multiply_reduce_fusion.6
  38.4 5.2 %fusion.94 = f32[48,8,16,16]{2,3,1,0:T(8,128)} fusion(bf16[48,16,8,72]{3,2,0,1:T(8,128)(2,1)S(1)} %copy-done.12, bf16[48,16,8,72]{3,2,0,1:T(8,128)(2,1)} %reshape.326), kind=kOutput, calls=%fused_computation.121 | convolution fusion | flops 14155776 | bytes 2162688 | tf_op jit(solution)/shard_map/blhd,bmhd->bhlm/dot_general | solution.py:76
  43.6 2.0 fusion.44
  47.2 2.6 fusion.82
  49.8 11.1 %fusion.38 = (f32[48,16,8]{1,2,0:T(8,128)}, f32[48,8,72,16]{2,3,1,0:T(8,128)}) fusion(f32[48,16,8,72]{3,2,1,0:T(8,128)} %reshape.338, f32[72]{0:T(128)S(1)} %copy-done.36, f32[48,8,16,16]{2,3,1,0:T(8,128)} %fusion.94, f32[48,8,16]{2,1,0:T(8,128)S(1)} %get-tuple-element.33, f32[48,8,16,16]{2,3,1,0:T(8,128)} %copy-done.18, f32[48,16,8,72]{3,2,1,0:T(8,128)} %reshape.337, ...), kind=kOutput, calls=%fused_computation.54 | convolution fusion | flops 17694736 | bytes 6169152 | tf_op jit(solution)/shard_map/bhlm,blhd->bmhd/dot_general | solution.py:87
  60.9 12.4 %fusion.41 = (f32[48,16,8]{1,2,0:T(8,128)}, f32[48,8,72,16]{2,3,1,0:T(8,128)}) fusion(f32[48,16,8,72]{3,2,1,0:T(8,128)} %reshape.337, f32[72]{0:T(128)S(1)} %copy-done.37, f32[48,8,16,16]{2,3,1,0:T(8,128)} %fusion.94, f32[48,8,16]{2,1,0:T(8,128)} %copy-done.24, f32[48,8,16,16]{2,3,1,0:T(8,128)} %copy-done.18, f32[48,16,8,72]{3,2,1,0:T(8,128)} %reshape.338, ...), kind=kOutput, calls=%fused_computation.59 | convolution fusion | flops 17694736 | bytes 6169152 | tf_op jit(solution)/shard_map/bhlm,bmhd->blhd/dot_general | solution.py:84
  77.9 3.0 copy.211
  80.9 3.7 %reshape.330 = bf16[48,16,576]{2,1,0:T(8,128)(2,1)} reshape(bf16[48,16,8,72]{3,2,1,0:T(8,128)(2,1)} %copy.211) | data formatting | bytes 1769472 | tf_op jit(solution)/shard_map/reshape | solution.py:95
  92.7 8.9 %fusion.37 = (bf16[48,16,8,72]{3,1,2,0:T(8,128)(2,1)S(1)}, bf16[48,16,8,72]{3,1,2,0:T(8,128)(2,1)}) fusion(f32[48,8,72,16]{2,3,1,0:T(8,128)} %get-tuple-element.38, f32[48,16,8,72]{3,2,1,0:T(8,128)} %reshape.338, f32[48,16,8]{1,2,0:T(8,128)} %copy.208, f32[48,16,8]{1,2,0:T(8,128)} %copy.204, f32[72]{0:T(128)} %get-tuple-element.30, ...), kind=kLoop, calls=%fused_computation.53 | loop fusion | flops 5308416 | bytes 8995392 | tf_op jit(solution)/shard_map/convert_element_type | solution.py:57
  103.2 3.7 %reshape.329 = bf16[48,16,576]{2,1,0:T(8,128)(2,1)} reshape(bf16[48,16,8,72]{3,2,1,0:T(8,128)(2,1)} %copy.209) | data formatting | bytes 1769472 | tf_op jit(solution)/shard_map/reshape | solution.py:57
  106.9 3.1 copy.203
  110.0 3.7 %reshape.328 = bf16[48,16,576]{2,1,0:T(8,128)(2,1)} reshape(bf16[48,16,8,72]{3,2,1,0:T(8,128)(2,1)} %copy.203) | data formatting | bytes 1769472 | tf_op jit(solution)/shard_map/reshape | solution.py:57
  113.6 5.6 %concatenate.13 = bf16[16,48,1728]{2,0,1:T(8,128)(2,1)} concatenate(bf16[16,48,576]{2,0,1:T(8,128)(2,1)} %bitcast.215, bf16[16,48,576]{2,0,1:T(8,128)(2,1)} %bitcast.214, bf16[16,48,576]{2,0,1:T(8,128)(2,1)} %bitcast.213), dimensions={2} | concatenate | bytes 5308416 | tf_op jit(solution)/shard_map/concatenate | solution.py:110
  119.2 2.7 copy.212
  122.2 5.5 %fusion.146 = (f32[1152]{0:T(1024)S(1)}, f32[768]{0:T(1024)S(1)}, f32[768,1152]{1,0:T(8,128)}) fusion(f32[1152]{0:T(1024)S(1)} %copy-done.29, bf16[768,1728]{1,0:T(8,128)(2,1)S(1)} %bitcast.222, bf16[1152,1728]{0,1:T(8,128)(2,1)S(1)} %copy-done.39), kind=kOutput, calls=%fused_computation.192 | convolution fusion | flops 3060300032 | bytes 10186752 | tf_op jit(solution)/shard_map/dot_general | solution.py:36
  127.8 3.3 fusion.23
  138.6 6.2 %all-to-all-start.1 = ((bf16[8,2,48,1152]{3,2,1,0:T(8,128)(2,1)}), bf16[8,2,48,1152]{3,2,1,0:T(8,128)(2,1)}, u32[]{:S(2)}, u32[]{:S(2)}) async-start(bf16[8,2,48,1152]{3,2,1,0:T(8,128)(2,1)} %fusion.116), calls=%async_computation.1 | async-start | bytes 3538944 | tf_op jit(solution)/shard_map/all_to_all | solution.py:12
  144.8 1.7 bitcast_convert_fusion
  149.4 1.8 copy-done.3
  152.8 3.9 %fusion.33 = bf16[2,384,1728]{1,2,0:T(8,128)(2,1)S(1)} fusion(bf16[2,384,1152]{2,1,0:T(8,128)(2,1)S(1)} %add_convert_fusion, bf16[1152,1728]{0,1:T(8,128)(2,1)S(1)} %copy-done.40), kind=kOutput, calls=%fused_computation.48 | convolution fusion | flops 3058974720 | bytes 8404992 | tf_op jit(solution)/shard_map/dot_general | solution.py:30
  158.3 27.2 %all-to-all-done.1 = bf16[8,2,48,1152]{3,2,1,0:T(8,128)(2,1)} async-done(((bf16[8,2,48,1152]{3,2,1,0:T(8,128)(2,1)}), bf16[8,2,48,1152]{3,2,1,0:T(8,128)(2,1)}, u32[]{:S(2)}, u32[]{:S(2)}) %all-to-all-start.1) | async-done | bytes 1769504 | tf_op jit(solution)/shard_map/all_to_all | solution.py:12
  185.5 1.7 convert_bitcast_fusion
  191.2 5.1 %fusion.156 = f32[2,8,384,384]{2,3,1,0:T(8,128)} fusion(bf16[2,384,8,72]{1,3,2,0:T(8,128)(2,1)S(1)} %bitcast.227, bf16[2,384,8,72]{1,3,2,0:T(8,128)(2,1)S(1)} %bitcast.220), kind=kOutput, calls=%fused_computation.195 | convolution fusion | flops 339738624 | bytes 11206656 | tf_op jit(solution)/shard_map/blhd,bmhd->bhlm/dot_general | solution.py:76
  196.3 1.9 fusion.4
  198.3 3.6 %copy-done.11 = f32[2,8,384,384]{2,3,1,0:T(8,128)} copy-done((f32[2,8,384,384]{2,3,1,0:T(8,128)}, f32[2,8,384,384]{2,3,1,0:T(8,128)S(1)}, u32[]{:S(2)}) %copy-start.11) | copy-done | bytes 9437208
  201.9 3.0 fusion.105
  204.9 18.2 %fusion.63 = (f32[2,384,8]{1,2,0:T(8,128)S(1)}, f32[2,8,72,384]{3,2,1,0:T(8,128)}) fusion(bf16[2,384,8,72]{1,3,2,0:T(8,128)(2,1)S(1)} %bitcast.205, f32[72]{0:T(128)S(1)} %copy-done.34, f32[2,8,384,384]{2,3,1,0:T(8,128)} %fusion.156, f32[2,8,384]{2,1,0:T(8,128)S(1)} %get-tuple-element.40, f32[2,8,384,384]{2,3,1,0:T(8,128)} %copy-done.11, ...), kind=kOutput, calls=%fused_computation.96 | convolution fusion | flops 364511616 | bytes 22487616 | tf_op jit(solution)/shard_map/bhlm,blhd->bmhd/dot_general | solution.py:87
  223.1 17.9 %fusion.70 = (f32[2,384,8]{1,2,0:T(8,128)S(1)}, f32[2,8,72,384]{3,2,1,0:T(8,128)}) fusion(bf16[2,384,8,72]{1,3,2,0:T(8,128)(2,1)S(1)} %bitcast.211, f32[72]{0:T(128)S(1)} %copy-done.35, f32[2,8,384,384]{2,3,1,0:T(8,128)} %fusion.156, f32[2,8,384]{2,1,0:T(8,128)S(1)} %get-tuple-element.40, f32[2,8,384,384]{2,3,1,0:T(8,128)} %copy-done.11, ...), kind=kOutput, calls=%fused_computation.103 | convolution fusion | flops 364511616 | bytes 22487616 | tf_op jit(solution)/shard_map/bhlm,bmhd->blhd/dot_general | solution.py:84
  240.9 2.2 copy.220
  248.0 6.2 %multiply_reduce_fusion.1 = (f32[1152]{0:T(1024)S(1)}, f32[768]{0:T(1024)S(1)}, f32[768]{0:T(1024)S(1)}, f32[1152]{0:T(1024)S(1)}, f32[768,1152]{1,0:T(8,128)}) fusion(f32[8,2,48,1152]{3,2,0,1:T(8,128)S(1)} %copy-done.4, f32[768]{0:T(1024)S(1)} %rsqrt.74, f32[768]{0:T(1024)S(1)} %div.96, f32[1152]{0:T(1024)S(1)} %copy-done.30, ...), kind=kOutput, calls=%fused_computation.43 | convolution fusion | flops 3073569280 | bytes 13739520 | tf_op jit(solution)/shard_map/dot_general | solution.py:36
  254.2 3.9 %multiply_convert_fusion.1 = bf16[2,384,1152]{2,1,0:T(8,128)(2,1)S(1)} fusion(f32[2,384,1152]{2,1,0:T(8,128)} %bitcast.219, f32[8,2,48,1152]{3,2,0,1:T(8,128)} %copy-done.3, f32[2,384]{1,0:T(2,128)S(1)} %div.98, f32[2,384]{1,0:T(2,128)S(1)} %div.95, f32[1152]{0:T(1024)S(1)} %copy-done.30, f32[2,384]{1,0:T(2,128)S(1)} %div.87, f32[2,384]{1,0:T(2,128)S(1)} %rsqrt.71), kind=kLoop, calls=%fused_computation.44 | loop fusion | flops 7077888 | bytes 8864256 | tf_op jit(solution)/shard_map/convert_element_type | solution.py:179
  258.1 3.0 copy.221
  261.1 4.3 %all-to-all-start.2 = ((bf16[2,384,1152]{2,0,1:T(2,128)(2,1)}), bf16[2,384,1152]{2,0,1:T(2,128)(2,1)}, u32[]{:S(2)}, u32[]{:S(2)}) async-start(bf16[2,384,1152]{2,0,1:T(2,128)(2,1)} %copy.221), calls=%async_computation.2 | async-start | bytes 3538944 | tf_op jit(solution)/shard_map/all_to_all | solution.py:180
  265.5 3.4 %fusion.83 = bf16[48,16,8,72]{3,1,2,0:T(8,128)(2,1)S(1)} fusion(bf16[48,16,8,72]{3,2,0,1:T(8,128)(2,1)S(1)} %copy-done.13, f32[48,8,16,16]{2,3,1,0:T(8,128)} %copy-done.18, f32[48,8,16]{2,1,0:T(8,128)S(1)} %copy-done.25), kind=kOutput, calls=%fused_computation.115 | convolution fusion | flops 14893056 | bytes 2187264 | tf_op jit(solution)/shard_map/bhlm,bmhd->blhd/dot_general | solution.py:73
  269.3 2.0 reshape.336
  271.3 3.5 %fusion.81 = f32[1152]{0:T(1024)S(1)} fusion(bf16[16,48,1152]{2,1,0:T(8,128)(2,1)} %param.13, bf16[576,1152]{1,0:T(8,128)(2,1)S(1)} %copy-done, bf16[16,48,576]{2,0,1:T(8,128)(2,1)} %bitcast.223), kind=kOutput, calls=%fused_computation.113 | convolution fusion | flops 1021868928 | bytes 3985920 | tf_op jit(solution)/shard_map/dot_general | solution.py:30
  274.9 5.6 %fusion.90 = bf16[2,8,72,384]{3,2,1,0:T(8,128)(2,1)S(1)} fusion(bf16[2,384,8,72]{1,3,2,0:T(8,128)(2,1)S(1)} %bitcast.221, f32[2,8,384,384]{2,3,1,0:T(8,128)} %copy-done.11, f32[2,8,384]{2,1,0:T(8,128)S(1)} %get-tuple-element.40), kind=kOutput, calls=%fused_computation.118 | convolution fusion | flops 347258880 | bytes 11231232 | tf_op jit(solution)/shard_map/bhlm,bmhd->blhd/dot_general | solution.py:73
  282.3 47.5 %psum.7 = f32[6,1152]{1,0:T(8,128)S(1)} all-reduce(f32[6,1152]{1,0:T(8,128)S(1)} %stack.63), channel_id=1, replica_groups=mesh['clip'=4,'seq'=8] {'seq'}, use_global_device_ids=true, to_apply=%region_26.0 | all-reduce | flops 6912 | bytes 55296 | tf_op jit(solution)/shard_map/psum | solution.py:191
  330.4 1.7 copy.222
  (163 shorter events, 46.6 us)
Async XLA Ops:
  0.6 8.9 %copy-start = (bf16[576,1152]{1,0:T(8,128)(2,1)S(1)}, bf16[576,1152]{1,0:T(8,128)(2,1)}, u32[]{:S(2)}) copy-start(bf16[576,1152]{1,0:T(8,128)(2,1)} %param.18) | copy-start | bytes 3981316
  0.6 7.6 %copy-start.38 = (f32[4,72]{1,0:T(4,128)S(1)}, f32[4,72]{1,0:T(4,128)}, u32[]{:S(2)}) copy-start(f32[4,72]{1,0:T(4,128)} %param.19) | copy-start | bytes 3460
  0.7 8.2 %copy-start.33 = (f32[5,1152]{1,0:T(8,128)S(1)}, f32[5,1152]{1,0:T(8,128)}, u32[]{:S(2)}) copy-start(f32[5,1152]{1,0:T(8,128)} %param.14) | copy-start | bytes 69124
  0.7 8.8 %copy-start.19 = (bf16[16,48,1152]{2,1,0:T(8,128)(2,1)S(1)}, bf16[16,48,1152]{2,1,0:T(8,128)(2,1)}, u32[]{:S(2)}) copy-start(bf16[16,48,1152]{2,1,0:T(8,128)(2,1)} %param.13) | copy-start | bytes 5308420
  0.7 137.9 %all-to-all-start = ((bf16[16,48,1152]{2,1,0:T(8,128)(2,1)}), bf16[16,48,1152]{2,1,0:T(8,128)(2,1)}, u32[]{:S(2)}, u32[]{:S(2)}) async-start(bf16[16,48,1152]{2,1,0:T(8,128)(2,1)} %param.10), calls=%async_computation | async-start | bytes 3538944 | tf_op jit(solution)/shard_map/all_to_all | solution.py:160
  23.0 3.9 %copy-start.15 = (bf16[48,16,576]{2,0,1:T(8,128)(2,1)S(1)}, bf16[48,16,576]{2,0,1:T(8,128)(2,1)}, u32[]{:S(2)}) copy-start(bf16[48,16,576]{2,0,1:T(8,128)(2,1)} %get-tuple-element.16) | copy-start | bytes 2654212
  34.4 3.9 %copy-start.12 = (bf16[48,16,8,72]{3,2,0,1:T(8,128)(2,1)S(1)}, bf16[48,16,8,72]{3,2,0,1:T(8,128)(2,1)}, u32[]{:S(2)}) copy-start(bf16[48,16,8,72]{3,2,0,1:T(8,128)(2,1)} %reshape.354) | copy-start | bytes 2654212
  38.3 5.2 %copy-start.1 = (f32[48,16,8,72]{3,2,1,0:T(8,128)S(1)}, f32[48,16,8,72]{3,2,1,0:T(8,128)}, u32[]{:S(2)}) copy-start(f32[48,16,8,72]{3,2,1,0:T(8,128)} %reshape.337) | copy-start | bytes 5308420
  38.3 5.2 %copy-start.2 = (f32[48,16,8,72]{3,2,1,0:T(8,128)S(1)}, f32[48,16,8,72]{3,2,1,0:T(8,128)}, u32[]{:S(2)}) copy-start(f32[48,16,8,72]{3,2,1,0:T(8,128)} %reshape.338) | copy-start | bytes 5308420
  38.3 5.2 %copy-start.36 = (f32[72]{0:T(128)S(1)}, f32[72]{0:T(128)}, u32[]{:S(2)}) copy-start(f32[72]{0:T(128)} %get-tuple-element.30) | copy-start | bytes 868
  38.4 5.2 %copy-start.37 = (f32[72]{0:T(128)S(1)}, f32[72]{0:T(128)}, u32[]{:S(2)}) copy-start(f32[72]{0:T(128)} %get-tuple-element.31) | copy-start | bytes 868
  43.6 3.7 %copy-start.14 = (bf16[48,16,8,72]{3,2,0,1:T(8,128)(2,1)S(1)}, bf16[48,16,8,72]{3,2,0,1:T(8,128)(2,1)}, u32[]{:S(2)}) copy-start(bf16[48,16,8,72]{3,2,0,1:T(8,128)(2,1)} %reshape.326) | copy-start | bytes 2654212
  45.6 1.6 copy-start.18
  45.6 4.2 %copy-start.24 = (f32[48,8,16]{2,1,0:T(8,128)}, f32[48,8,16]{2,1,0:T(8,128)S(1)}, u32[]{:S(2)}) copy-start(f32[48,8,16]{2,1,0:T(8,128)S(1)} %get-tuple-element.33) | copy-start | bytes 73732
  60.9 12.4 %copy-start.5 = (bf16[16,48,1152]{2,1,0:T(8,128)(2,1)S(1)}, bf16[16,48,1152]{2,1,0:T(8,128)(2,1)}, u32[]{:S(2)}) copy-start(bf16[16,48,1152]{2,1,0:T(8,128)(2,1)} %param.11) | copy-start | bytes 5308420
  73.3 2.1 copy-start.23
  73.6 0.6 copy-start.26
  119.2 2.7 copy-start.29
  119.2 3.0 copy-start.39
  122.2 5.6 %copy-start.27 = (f32[16,48]{1,0:T(8,128)S(1)}, f32[16,48]{1,0:T(8,128)}, u32[]{:S(2)}) copy-start(f32[16,48]{1,0:T(8,128)} %copy-done.26) | copy-start | bytes 9220
  122.2 5.6 %copy-start.28 = (f32[16,48]{1,0:T(8,128)S(1)}, f32[16,48]{1,0:T(8,128)}, u32[]{:S(2)}) copy-start(f32[16,48]{1,0:T(8,128)} %add_rsqrt_fusion.5) | copy-start | bytes 9220
  127.8 3.4 %copy-start.8 = (f32[768,1152]{1,0:T(8,128)S(1)}, f32[768,1152]{1,0:T(8,128)}, u32[]{:S(2)}) copy-start(f32[768,1152]{1,0:T(8,128)} %get-tuple-element.39) | copy-start | bytes 10616836
  127.8 3.6 %copy-start.20 = (bf16[16,48,1152]{2,1,0:T(8,128)(2,1)S(1)}, bf16[16,48,1152]{2,1,0:T(8,128)(2,1)}, u32[]{:S(2)}) copy-start(bf16[16,48,1152]{2,1,0:T(8,128)(2,1)} %param.13) | copy-start | bytes 5308420
  132.9 5.0 %copy-start.6 = (bf16[16,48,1152]{2,1,0:T(8,128)(2,1)}, bf16[16,48,1152]{2,1,0:T(8,128)(2,1)S(1)}, u32[]{:S(2)}) copy-start(bf16[16,48,1152]{2,1,0:T(8,128)(2,1)S(1)} %fusion.26) | copy-start | bytes 5308420
  138.6 46.9 %all-to-all-start.1 = ((bf16[8,2,48,1152]{3,2,1,0:T(8,128)(2,1)}), bf16[8,2,48,1152]{3,2,1,0:T(8,128)(2,1)}, u32[]{:S(2)}, u32[]{:S(2)}) async-start(bf16[8,2,48,1152]{3,2,1,0:T(8,128)(2,1)} %fusion.116), calls=%async_computation.1 | async-start | bytes 3538944 | tf_op jit(solution)/shard_map/all_to_all | solution.py:12
  147.3 3.9 %copy-start.30 = (f32[1152]{0:T(1024)S(1)}, f32[1152]{0:T(1024)}, u32[]{:S(2)}) copy-start(f32[1152]{0:T(1024)} %get-tuple-element.10) | copy-start | bytes 13828
  147.3 3.9 %copy-start.32 = (f32[1152]{0:T(1024)S(1)}, f32[1152]{0:T(1024)}, u32[]{:S(2)}) copy-start(f32[1152]{0:T(1024)} %get-tuple-element.14) | copy-start | bytes 13828
  149.4 1.8 copy-start.3
  149.4 3.4 %copy-start.40 = (bf16[1152,1728]{0,1:T(8,128)(2,1)S(1)}, bf16[1152,1728]{0,1:T(8,128)(2,1)}, u32[]{:S(2)}) copy-start(bf16[1152,1728]{0,1:T(8,128)(2,1)} %param.15) | copy-start | bytes 11943940
  187.2 0.7 copy-start.31
  187.5 3.7 %copy-start.9 = (f32[2,8,48,1152]{3,2,1,0:T(8,128)}, f32[2,8,48,1152]{3,2,1,0:T(8,128)S(1)}, u32[]{:S(2)}) copy-start(f32[2,8,48,1152]{3,2,1,0:T(8,128)S(1)} %copy.214) | copy-start | bytes 10616836
  187.5 2.3 copy-start.42
  189.8 1.4 copy-start.16
  191.2 5.1 %copy-start.34 = (f32[72]{0:T(128)S(1)}, f32[72]{0:T(128)}, u32[]{:S(2)}) copy-start(f32[72]{0:T(128)} %get-tuple-element.29) | copy-start | bytes 868
  191.2 5.1 %copy-start.35 = (f32[72]{0:T(128)S(1)}, f32[72]{0:T(128)}, u32[]{:S(2)}) copy-start(f32[72]{0:T(128)} %get-tuple-element.32) | copy-start | bytes 868
  198.3 3.6 %copy-start.11 = (f32[2,8,384,384]{2,3,1,0:T(8,128)}, f32[2,8,384,384]{2,3,1,0:T(8,128)S(1)}, u32[]{:S(2)}) copy-start(f32[2,8,384,384]{2,3,1,0:T(8,128)S(1)} %get-tuple-element.41) | copy-start | bytes 28311556
  240.9 2.4 copy-start.22
  243.3 1.6 copy-start.21
  244.8 2.1 copy-start.41
  245.0 3.0 copy-start.4
  258.1 7.4 %copy-start.13 = (bf16[48,16,8,72]{3,2,0,1:T(8,128)(2,1)S(1)}, bf16[48,16,8,72]{3,2,0,1:T(8,128)(2,1)}, u32[]{:S(2)}) copy-start(bf16[48,16,8,72]{3,2,0,1:T(8,128)(2,1)} %reshape.354) | copy-start | bytes 2654212
  258.1 7.4 %copy-start.25 = (f32[48,8,16]{2,1,0:T(8,128)S(1)}, f32[48,8,16]{2,1,0:T(8,128)}, u32[]{:S(2)}) copy-start(f32[48,8,16]{2,1,0:T(8,128)} %copy-done.24) | copy-start | bytes 73732
  261.1 69.3 %all-to-all-start.2 = ((bf16[2,384,1152]{2,0,1:T(2,128)(2,1)}), bf16[2,384,1152]{2,0,1:T(2,128)(2,1)}, u32[]{:S(2)}, u32[]{:S(2)}) async-start(bf16[2,384,1152]{2,0,1:T(2,128)(2,1)} %copy.221), calls=%async_computation.2 | async-start | bytes 3538944 | tf_op jit(solution)/shard_map/all_to_all | solution.py:180
  271.3 3.5 %copy-start.17 = (bf16[2,384,576]{1,2,0:T(8,128)(2,1)S(1)}, bf16[2,384,576]{1,2,0:T(8,128)(2,1)}, u32[]{:S(2)}) copy-start(bf16[2,384,576]{1,2,0:T(8,128)(2,1)} %get-tuple-element.18) | copy-start | bytes 2654212
  274.8 5.6 %copy-start.10 = (f32[2,8,48,1152]{3,2,1,0:T(8,128)S(1)}, f32[2,8,48,1152]{3,2,1,0:T(8,128)}, u32[]{:S(2)}) copy-start(f32[2,8,48,1152]{3,2,1,0:T(8,128)} %copy-done.9) | copy-start | bytes 10616836
  274.8 5.6 %copy-start.43 = (bf16[576,1152]{1,0:T(8,128)(2,1)S(1)}, bf16[576,1152]{1,0:T(8,128)(2,1)}, u32[]{:S(2)}) copy-start(bf16[576,1152]{1,0:T(8,128)(2,1)} %param.16) | copy-start | bytes 3981316
  282.2 50.0 %copy-start.7 = (bf16[16,48,1152]{2,1,0:T(8,128)(2,1)S(1)}, bf16[16,48,1152]{2,1,0:T(8,128)(2,1)}, u32[]{:S(2)}) copy-start(bf16[16,48,1152]{2,1,0:T(8,128)(2,1)} %copy-done.6) | copy-start | bytes 5308420
